TPU v7x, 32 devices: a whole 2x2x4 slice. The times are simulated.
32 devices in a mesh: variant: 4 (over x, core), mesh: 8 (over z, y).
Axes of the slice: x: 2, y: 2, z: 4, core: 2. Of those that a mesh axis runs over, the one named last changes fastest.
Arguments:
- snapshots: float32 [4, 64, 131072], P('variant', None, 'mesh'), may hold values from -12 to 12, as said below
- ref_index: int32 [1], replicated, may hold values from 0 to 3
- weight_codes: int32 [4], replicated, may hold values from 1 to 16
Outputs:
- new_basis: float32 [64, 131072], P(None, 'mesh')
Inputs may be any that keep to these rules, and one draw needn't show every extreme that they name: `snapshots`: each variant's snapshot matrix has full rank 64, and the principal angles between any two variants' spans have tangents below 0.8.
All inputs are finite; a program needn't handle non-finite values.
Results may differ from a plain program's by a relative error of at most 0.0001.
Values sent between devices are 32-bit elements; how exact they have to be, the bound alone decides.
No kernel may reach another device: no remote copies, remote signals or barrier semaphores. Data moves between devices by JAX's collectives and lax.ppermute only.
A program may use at most 64 MiB of HBM per device.

v0:
```python
import math
import jax
import jax.numpy as jnp
from jax import lax
from jax.sharding import PartitionSpec as P

highest = lax.Precision.HIGHEST
atan_coeffs = [(-1.0) ** k / (2 * k + 1) for k in range(24)]
cos_coeffs = [(-1.0) ** k / math.factorial(2 * k) for k in range(24)]
sin_coeffs = [(-1.0) ** k / math.factorial(2 * k + 1) for k in range(24)]


def broadcast(x, axis, root):
    mine = lax.axis_index(axis) == root
    return lax.psum(jnp.where(mine, x, jnp.zeros_like(x)), axis)


def product(left, right):
    return jnp.dot(left, right, precision=highest, preferred_element_type=jnp.float32)


def series(matrix, coeffs):
    eye = jnp.eye(matrix.shape[0], dtype=jnp.float32)
    total = coeffs[-1] * eye
    for coeff in reversed(coeffs[:-1]):
        total = coeff * eye + product(matrix, total)
    return total


def inverse(matrix):
    factor = jnp.linalg.cholesky(product(matrix.T, matrix))
    return jax.scipy.linalg.cho_solve((factor, True), matrix.T)


def on_device(snapshots, ref_index, weight_codes):
    own_snap = snapshots[0]
    root = ref_index[0]
    codes = weight_codes.astype(jnp.float32)
    weight = codes[lax.axis_index("variant")] / jnp.sum(codes)
    eye = jnp.eye(own_snap.shape[0], dtype=jnp.float32)
    scale = jnp.float32(math.sqrt(own_snap.shape[1] * lax.axis_size("mesh")))
    gram_own = lax.psum(product(own_snap, own_snap.T), "mesh")
    lower_own = jnp.linalg.cholesky(gram_own)
    base_own = jax.scipy.linalg.solve_triangular(lower_own, own_snap, lower=True)
    base_ref = broadcast(base_own, "variant", root)
    correlation = lax.psum(product(base_ref, base_own.T), "mesh")
    minv = inverse(correlation)
    tangent = product(minv.T, base_own) - base_ref
    tangent_gram = product(minv.T, minv) - eye
    term = weight * product(series(tangent_gram, atan_coeffs), tangent)
    blended = lax.psum(term, "variant")
    energy = lax.psum(product(blended, blended.T), "mesh")
    mixed = product(series(energy, cos_coeffs), base_ref) + product(
        series(energy, sin_coeffs), blended
    )
    return mixed * scale


def solution(mesh):
    return jax.shard_map(
        on_device,
        mesh=mesh,
        in_specs=(P("variant", None, "mesh"), P(), P()),
        out_specs=P(None, "mesh"),
        check_vma=False,
    )
```

profile of v0, /device:TPU:0, one launch (start us, length us, event | category | flops | bytes accessed | tf_op | source)
XLA Modules:
  0.0 382.1 jit_solution(7541241715108822365)
XLA Ops:
  6.5 6.9 %fusion.3 = f32[64,64]{0,1:T(8,128)S(1)} fusion(f32[1,64,16384]{2,1,0:T(8,128)} %param.4), kind=kOutput, calls=%fused_computation.6 | convolution fusion | flops 805306368 | bytes 4210688 | tf_op jit(solution)/shard_map/dot_general | solution.py:19
  13.5 38.9 %psum.35 = f32[64,64]{0,1:T(8,128)S(1)} all-reduce(f32[64,64]{0,1:T(8,128)S(1)} %fusion.3), channel_id=1, replica_groups=mesh['variant'=4,'mesh'=8] {'mesh'}, use_global_device_ids=true, to_apply=%region_1.0 | all-reduce | flops 4096 | bytes 32768 | tf_op jit(solution)/shard_map/psum | solution.py:42
  52.5 5.8 %cholesky.44 = f32[64,64]{1,0:T(8,128)S(1)} custom-call(f32[64,64]{1,0:T(8,128)S(1)} %fusion.15), custom_call_target="Cholesky" | custom-call | tf_op jit(solution)/shard_map/jit(cholesky)/cholesky | solution.py:43
  58.4 0.6 compare_reduce_fusion.1
  59.0 0.7 fusion.7
  59.7 4.9 %custom-call.13 = f32[1,64,64]{1,2,0:T(8,128)S(1)} custom-call(f32[1,64,64]{2,1,0:T(8,128)S(1)} %fusion.7), custom_call_target="InvertDiagBlocksLowerTriangular" | custom-call | tf_op jit(solution)/shard_map/jit(_solve_triangular)/triangular_solve | solution.py:44
  65.2 9.3 %broadcast_select_fusion = (f32[64,16384]{1,0:T(8,128)}, f32[64,16384]{1,0:T(8,128)}) fusion(pred[]{:T(512)S(6)} %eq.142, f32[1,64,16384]{2,1,0:T(8,128)} %param.4, f32[1,64,64]{1,2,0:T(8,128)S(1)} %custom-call.13), kind=kOutput, calls=%fused_computation.8 | convolution fusion | flops 806354944 | bytes 12599297 | tf_op jit(solution)/shard_map/jit(_solve_triangular)/triangular_solve | solution.py:44
  74.5 0.2 all-reduce.5.cloned.1.call-start
  74.8 0.4 copy-done.1
  75.2 0.6 dynamic_slice.3
  75.7 0.6 convert_reduce_fusion
  77.6 79.8 %all-reduce.3.cloned.1.call-done = f32[64,16384]{1,0:T(8,128)} async-done(((f32[64,16384]{1,0:T(8,128)}), f32[64,16384]{1,0:T(8,128)}) %all-reduce.3.cloned.1.call-update) | async-done | bytes 4194320 | tf_op jit(solution)/shard_map/psum | solution.py:15
  157.4 6.9 %fusion.35 = f32[64,64]{1,0:T(8,128)S(1)} fusion(f32[64,16384]{1,0:T(8,128)} %all-reduce.3.cloned.1.call-done, f32[64,16384]{1,0:T(8,128)} %get-tuple-element.7), kind=kOutput, calls=%fused_computation.114 | convolution fusion | flops 805306368 | bytes 8404992 | tf_op jit(solution)/shard_map/dot_general | solution.py:19
  164.4 37.1 %psum.37 = f32[64,64]{1,0:T(8,128)S(1)} all-reduce(f32[64,64]{1,0:T(8,128)S(1)} %fusion.35), channel_id=1, replica_groups=mesh['variant'=4,'mesh'=8] {'mesh'}, use_global_device_ids=true, to_apply=%region_5.7 | all-reduce | flops 4096 | bytes 32768 | tf_op jit(solution)/shard_map/psum | solution.py:46
  201.5 0.2 fusion.36
  201.8 5.8 %cholesky.55 = f32[64,64]{1,0:T(8,128)S(1)} custom-call(f32[64,64]{1,0:T(8,128)S(1)} %fusion.13), custom_call_target="Cholesky" | custom-call | tf_op jit(solution)/shard_map/jit(cholesky)/cholesky | solution.py:31
  207.7 0.6 compare_reduce_fusion
  208.3 0.7 fusion.8
  209.0 4.9 %custom-call.14 = f32[1,64,64]{1,2,0:T(8,128)S(1)} custom-call(f32[1,64,64]{2,1,0:T(8,128)S(1)} %fusion.8), custom_call_target="InvertDiagBlocksLowerTriangular" | custom-call | tf_op jit(solution)/shard_map/jit(_cho_solve)/triangular_solve | solution.py:32
  213.9 0.2 fusion.11
  214.3 0.2 convolution_subtract_fusion.1
  214.5 0.2 convolution_add_fusion.62
  215.2 0.2 convolution_add_fusion.58
  215.4 0.2 convolution_add_fusion.57
  215.9 0.2 convolution_add_fusion.54
  216.8 0.2 convolution_add_fusion.49
  216.9 0.2 convolution_add_fusion.48
  217.8 0.2 convolution_add_fusion.43
  218.3 0.2 convolution_add_fusion.40
  218.5 7.2 %convolution_subtract_fusion = f32[64,16384]{1,0:T(8,128)S(1)} fusion(f32[64,16384]{1,0:T(8,128)} %all-reduce.3.cloned.1.call-done, f32[64,64]{1,0:T(8,128)S(1)} %fusion.9, f32[64,16384]{1,0:T(8,128)} %get-tuple-element.7), kind=kOutput, calls=%fused_computation.3 | convolution fusion | flops 806354944 | bytes 12599296 | tf_op jit(solution)/shard_map/dot_general | solution.py:19
  225.7 5.2 %convolution_multiply_fusion = f32[64,16384]{1,0:T(8,128)} fusion(f32[64,64]{1,0:T(8,128)S(1)} %convolution_add_fusion.40, f32[64,16384]{1,0:T(8,128)S(1)} %convolution_subtract_fusion, f32[]{:T(128)S(6)} %div.9), kind=kOutput, calls=%fused_computation.2 | convolution fusion | flops 806354944 | bytes 8404996 | tf_op jit(solution)/shard_map/dot_general | solution.py:19
  230.9 82.1 %all-reduce.5.cloned.1.call-done = f32[64,16384]{1,0:T(8,128)} async-done(((f32[64,16384]{1,0:T(8,128)}), f32[64,16384]{1,0:T(8,128)}) %all-reduce.5.cloned.1.call-update) | async-done | bytes 4194320 | tf_op jit(solution)/shard_map/psum | solution.py:51
  313.0 6.9 %fusion.37 = f32[64,64]{1,0:T(8,128)S(1)} fusion(f32[64,16384]{1,0:T(8,128)} %all-reduce.5.cloned.1.call-done), kind=kOutput, calls=%fused_computation.116 | convolution fusion | flops 805306368 | bytes 4210688 | tf_op jit(solution)/shard_map/dot_general | solution.py:19
  320.0 37.1 %psum.39 = f32[64,64]{1,0:T(8,128)S(1)} all-reduce(f32[64,64]{1,0:T(8,128)S(1)} %fusion.37), channel_id=1, replica_groups=mesh['variant'=4,'mesh'=8] {'mesh'}, use_global_device_ids=true, to_apply=%region_7.9 | all-reduce | flops 4096 | bytes 32768 | tf_op jit(solution)/shard_map/psum | solution.py:52
  357.1 0.2 fusion.5
  357.7 0.2 convolution_add_fusion.19
  357.9 0.2 convolution_add_fusion.38
  358.6 0.2 convolution_add_fusion.15
  359.1 0.2 convolution_add_fusion.12
  360.0 0.2 convolution_add_fusion.7
  360.1 0.2 convolution_add_fusion.6
  361.5 0.2 convolution_add_fusion.35
  362.5 0.2 convolution_add_fusion.29
  363.2 0.2 convolution_add_fusion.25
  363.9 0.2 convolution_add_fusion.21
  364.0 0.2 convolution_add_fusion.20
  364.2 5.6 %fusion.40 = f32[64,16384]{1,0:T(8,128)S(1)} fusion(f32[64,64]{1,0:T(8,128)S(1)} %convolution_add_fusion.20, f32[64,16384]{1,0:T(8,128)} %all-reduce.3.cloned.1.call-done), kind=kOutput, calls=%fused_computation.119 | convolution fusion | flops 805306368 | bytes 8404992 | tf_op jit(solution)/shard_map/dot_general | solution.py:19
  369.9 5.4 %fusion = f32[64,16384]{1,0:T(8,128)} fusion(f32[64,16384]{1,0:T(8,128)S(1)} %fusion.40, f32[64,64]{1,0:T(8,128)S(1)} %convolution_add_fusion.1, f32[64,16384]{1,0:T(8,128)S(1)} %copy-done), kind=kOutput, calls=%fused_computation.1 | convolution fusion | flops 807403520 | bytes 12599296 | tf_op jit(solution)/shard_map/dot_general | solution.py:19
  (59 shorter events, 7.7 us)
Async XLA Ops:
  6.5 150.9 %all-reduce.3.cloned.1.call-start = ((), (), s32[]{:S(2)}) async-start(), calls=%async_computation | async-start | bytes 8388608 | tf_op jit(solution)/shard_map/psum | solution.py:15
  74.5 0.7 copy-start.1
  74.5 238.5 %all-reduce.5.cloned.1.call-start = ((), (), s32[]{:S(2)}) async-start(), calls=%async_computation.1 | async-start | bytes 8388608 | tf_op jit(solution)/shard_map/psum | solution.py:51
  364.2 5.6 %copy-start = (f32[64,16384]{1,0:T(8,128)S(1)}, f32[64,16384]{1,0:T(8,128)}, u32[]{:S(2)}) copy-start(f32[64,16384]{1,0:T(8,128)} %all-reduce.5.cloned.1.call-done) | copy-start | bytes 12582916
Sparse Core Ops, SparseCore 0:
  74.7 82.7 all-reduce.2
  231.0 81.9 all-reduce.4
where the time goes:
time: 382 us
  waiting for transfers between devices  162 us (42%)
  blocking collectives  113 us (30%)
  matrix products  64.9 us (17%)
  other arithmetic  24.8 us (6%)
  between operations  15.9 us (4%)
    psum x1, waiting for transfers between devices, on_device(): blended = lax.psum(term, 'variant')  82.1 us
    psum x1, waiting for transfers between devices, broadcast(): return lax.psum(jnp.where(mine, x, jnp.zeros_like(x)), axis)  79.8 us
    dot_general x74, matrix products, product(): jnp.dot(left, right, precision=highest, preferred_element_type=jnp.float32)  55.2 us
    psum x1, blocking collectives, on_device(): gram_own = lax.psum(product(own_snap, own_snap.T), 'mesh')  38.9 us
    psum x1, blocking collectives, on_device(): energy = lax.psum(product(blended, blended.T), 'mesh')  37.1 us
    psum x1, blocking collectives, on_device(): correlation = lax.psum(product(base_ref, base_own.T), 'mesh')  37.1 us
    another operation x1, matrix products, on_device(): jax.scipy.linalg.solve_triangular(lower_own, own_snap, lower=True)  9.28 us
  transfers between devices with their start and end apart: 2, of which 2 were waited for; matrix products, arithmetic and copies ran while one was open for 0% of the time, Pallas kernels for 0%

commit v1 on v0

--- a/solution.py
+++ b/solution.py
@@ -48,7 +48,9 @@
     tangent = product(minv.T, base_own) - base_ref
     tangent_gram = product(minv.T, minv) - eye
     term = weight * product(series(tangent_gram, atan_coeffs), tangent)
-    blended = lax.psum(term, "variant")
+    blended = term
+    for hop in (1, 2):
+        blended = blended + lax.ppermute(blended, "variant", [(dev, dev ^ hop) for dev in range(4)])
     energy = lax.psum(product(blended, blended.T), "mesh")
     mixed = product(series(energy, cos_coeffs), base_ref) + product(
         series(energy, sin_coeffs), blended

time: 382 us -> 394 us (1.031)
  waiting for transfers between devices: 162 us -> 179 us
  matrix products: 64.9 us -> 60.2 us
  blocking collectives: 113 us -> 109 us
    ppermute x0 -> x2, waiting for transfers between devices: none -> 99.1 us  [on_device(): lax.ppermute(blended, 'variant', [(dev, dev ^ hop) for dev in range(4)])]
    psum x1 -> x0, waiting for transfers between devices: 82.1 us -> none  [on_device(): blended = lax.psum(term, 'variant')]
    dot_general x74, matrix products: 55.2 us -> 50.5 us  [product(): jnp.dot(left, right, precision=highest, preferred_element_type=jnp.float32)]
    psum x1, blocking collectives: 37.1 us -> 33 us  [on_device(): energy = lax.psum(product(blended, blended.T), 'mesh')]
  transfers between devices with their start and end apart: 2 -> 3, of which waited for: 2 -> 3; matrix products, arithmetic and copies ran while one was open for 0% -> 0% of each run, Pallas kernels for 0% -> 0%
where the time goes in v1:
time: 394 us
  waiting for transfers between devices  179 us (45%)
  blocking collectives  109 us (28%)
  matrix products  60.2 us (15%)
  other arithmetic  25.9 us (7%)
  between operations  16 us (4%)
    ppermute x2, waiting for transfers between devices, on_device(): lax.ppermute(blended, 'variant', [(dev, dev ^ hop) for dev in range(4)])  99.1 us
    psum x1, waiting for transfers between devices, broadcast(): return lax.psum(jnp.where(mine, x, jnp.zeros_like(x)), axis)  79.8 us
    dot_general x74, matrix products, product(): jnp.dot(left, right, precision=highest, preferred_element_type=jnp.float32)  50.5 us
    psum x1, blocking collectives, on_device(): gram_own = lax.psum(product(own_snap, own_snap.T), 'mesh')  38.9 us
    psum x1, blocking collectives, on_device(): correlation = lax.psum(product(base_ref, base_own.T), 'mesh')  37.1 us
    psum x1, blocking collectives, on_device(): energy = lax.psum(product(blended, blended.T), 'mesh')  33 us
    another operation x1, matrix products, on_device(): jax.scipy.linalg.solve_triangular(lower_own, own_snap, lower=True)  9.28 us
  transfers between devices with their start and end apart: 3, of which 3 were waited for; matrix products, arithmetic and copies ran while one was open for 0% of the time, Pallas kernels for 0%

profile of v1, /device:TPU:0, one launch (start us, length us, event | category | flops | bytes accessed | tf_op | source)
XLA Modules:
  0.0 394.2 jit_solution(16355510184651458519)
XLA Ops:
  6.5 6.9 %fusion.3 = f32[64,64]{0,1:T(8,128)S(1)} fusion(f32[1,64,16384]{2,1,0:T(8,128)} %param.4), kind=kOutput, calls=%fused_computation.6 | convolution fusion | flops 805306368 | bytes 4210688 | tf_op jit(solution)/shard_map/dot_general | solution.py:19
  13.5 38.9 %psum.28 = f32[64,64]{0,1:T(8,128)S(1)} all-reduce(f32[64,64]{0,1:T(8,128)S(1)} %fusion.3), channel_id=1, replica_groups=mesh['variant'=4,'mesh'=8] {'mesh'}, use_global_device_ids=true, to_apply=%region_1.0 | all-reduce | flops 4096 | bytes 32768 | tf_op jit(solution)/shard_map/psum | solution.py:42
  52.5 5.8 %cholesky.44 = f32[64,64]{1,0:T(8,128)S(1)} custom-call(f32[64,64]{1,0:T(8,128)S(1)} %fusion.15), custom_call_target="Cholesky" | custom-call | tf_op jit(solution)/shard_map/jit(cholesky)/cholesky | solution.py:43
  58.4 0.6 compare_reduce_fusion.1
  59.0 0.7 fusion.7
  59.7 4.9 %custom-call.13 = f32[1,64,64]{1,2,0:T(8,128)S(1)} custom-call(f32[1,64,64]{2,1,0:T(8,128)S(1)} %fusion.7), custom_call_target="InvertDiagBlocksLowerTriangular" | custom-call | tf_op jit(solution)/shard_map/jit(_solve_triangular)/triangular_solve | solution.py:44
  65.3 9.3 %broadcast_select_fusion = (f32[64,16384]{1,0:T(8,128)}, f32[64,16384]{1,0:T(8,128)}) fusion(pred[]{:T(512)S(6)} %eq.142, f32[1,64,16384]{2,1,0:T(8,128)} %param.4, f32[1,64,64]{1,2,0:T(8,128)S(1)} %custom-call.13), kind=kOutput, calls=%fused_computation.8 | convolution fusion | flops 806354944 | bytes 12599297 | tf_op jit(solution)/shard_map/jit(_solve_triangular)/triangular_solve | solution.py:44
  74.6 0.6 copy-done.2
  75.2 0.6 dynamic_slice.3
  75.8 0.6 convert_reduce_fusion
  77.6 79.8 %all-reduce.2.cloned.1.call-done = f32[64,16384]{1,0:T(8,128)} async-done(((f32[64,16384]{1,0:T(8,128)}), f32[64,16384]{1,0:T(8,128)}) %all-reduce.2.cloned.1.call-update) | async-done | bytes 4194320 | tf_op jit(solution)/shard_map/psum | solution.py:15
  157.5 6.9 %fusion.35 = f32[64,64]{1,0:T(8,128)S(1)} fusion(f32[64,16384]{1,0:T(8,128)} %all-reduce.2.cloned.1.call-done, f32[64,16384]{1,0:T(8,128)} %get-tuple-element.7), kind=kOutput, calls=%fused_computation.114 | convolution fusion | flops 805306368 | bytes 8404992 | tf_op jit(solution)/shard_map/dot_general | solution.py:19
  164.4 37.1 %psum.30 = f32[64,64]{1,0:T(8,128)S(1)} all-reduce(f32[64,64]{1,0:T(8,128)S(1)} %fusion.35), channel_id=1, replica_groups=mesh['variant'=4,'mesh'=8] {'mesh'}, use_global_device_ids=true, to_apply=%region_5.7 | all-reduce | flops 4096 | bytes 32768 | tf_op jit(solution)/shard_map/psum | solution.py:46
  201.5 0.2 fusion.36
  201.8 5.8 %cholesky.55 = f32[64,64]{1,0:T(8,128)S(1)} custom-call(f32[64,64]{1,0:T(8,128)S(1)} %fusion.13), custom_call_target="Cholesky" | custom-call | tf_op jit(solution)/shard_map/jit(cholesky)/cholesky | solution.py:31
  207.7 0.6 compare_reduce_fusion
  208.4 0.7 fusion.8
  209.0 4.9 %custom-call.14 = f32[1,64,64]{1,2,0:T(8,128)S(1)} custom-call(f32[1,64,64]{2,1,0:T(8,128)S(1)} %fusion.8), custom_call_target="InvertDiagBlocksLowerTriangular" | custom-call | tf_op jit(solution)/shard_map/jit(_cho_solve)/triangular_solve | solution.py:32
  213.9 0.2 fusion.11
  214.3 0.2 convolution_subtract_fusion.1
  214.6 0.2 convolution_add_fusion.62
  214.9 0.2 convolution_add_fusion.60
  215.9 0.2 convolution_add_fusion.54
  216.6 0.2 convolution_add_fusion.50
  217.3 0.2 convolution_add_fusion.46
  217.5 0.2 convolution_add_fusion.45
  218.3 0.2 convolution_add_fusion.40
  218.5 7.2 %convolution_subtract_fusion = f32[64,16384]{1,0:T(8,128)S(1)} fusion(f32[64,16384]{1,0:T(8,128)} %all-reduce.2.cloned.1.call-done, f32[64,64]{1,0:T(8,128)S(1)} %fusion.9, f32[64,16384]{1,0:T(8,128)} %get-tuple-element.7), kind=kOutput, calls=%fused_computation.3 | convolution fusion | flops 806354944 | bytes 12599296 | tf_op jit(solution)/shard_map/dot_general | solution.py:19
  225.7 4.0 %convolution_multiply_fusion = f32[64,16384]{1,0:T(8,128)S(1)} fusion(f32[64,64]{1,0:T(8,128)S(1)} %convolution_add_fusion.40, f32[64,16384]{1,0:T(8,128)S(1)} %convolution_subtract_fusion, f32[]{:T(128)S(6)} %div.9), kind=kOutput, calls=%fused_computation.2 | convolution fusion | flops 806354944 | bytes 8404996 | tf_op jit(solution)/shard_map/dot_general | solution.py:19
  229.8 7.1 %collective-permute-done = f32[64,16384]{1,0:T(8,128)S(1)} collective-permute-done((f32[64,16384]{1,0:T(8,128)S(1)}, f32[64,16384]{1,0:T(8,128)S(1)}, u32[]{:S(2)}, u32[]{:S(2)}) %collective-permute-start) | collective-permute-done | bytes 4194336 | tf_op jit(solution)/shard_map/ppermute | solution.py:53
  236.9 0.4 add.257
  237.3 0.8 collective-permute-start.1
  238.1 91.9 %collective-permute-done.1 = f32[64,16384]{1,0:T(8,128)S(1)} collective-permute-done((f32[64,16384]{1,0:T(8,128)S(1)}, f32[64,16384]{1,0:T(8,128)S(1)}, u32[]{:S(2)}, u32[]{:S(2)}) %collective-permute-start.1) | collective-permute-done | bytes 4194336 | tf_op jit(solution)/shard_map/ppermute | solution.py:53
  330.0 0.7 add.258
  330.7 2.0 copy-done
  332.7 3.4 fusion.37
  336.1 33.0 %psum.31 = f32[64,64]{1,0:T(8,128)S(1)} all-reduce(f32[64,64]{1,0:T(8,128)S(1)} %fusion.37), channel_id=1, replica_groups=mesh['variant'=4,'mesh'=8] {'mesh'}, use_global_device_ids=true, to_apply=%region_6.8 | all-reduce | flops 4096 | bytes 32768 | tf_op jit(solution)/shard_map/psum | solution.py:54
  369.1 0.2 fusion.5
  369.8 0.2 convolution_add_fusion.19
  370.0 0.2 convolution_add_fusion.38
  370.7 0.2 convolution_add_fusion.15
  371.3 0.2 convolution_add_fusion.11
  372.0 0.2 convolution_add_fusion.7
  372.2 0.2 convolution_add_fusion.6
  373.1 0.2 convolution_add_fusion.1
  373.7 0.2 convolution_add_fusion.34
  376.3 5.6 %fusion.40 = f32[64,16384]{1,0:T(8,128)S(1)} fusion(f32[64,64]{1,0:T(8,128)S(1)} %convolution_add_fusion.20, f32[64,16384]{1,0:T(8,128)} %all-reduce.2.cloned.1.call-done), kind=kOutput, calls=%fused_computation.119 | convolution fusion | flops 805306368 | bytes 8404992 | tf_op jit(solution)/shard_map/dot_general | solution.py:19
  381.9 5.4 %fusion = f32[64,16384]{1,0:T(8,128)} fusion(f32[64,16384]{1,0:T(8,128)S(1)} %fusion.40, f32[64,64]{1,0:T(8,128)S(1)} %convolution_add_fusion.1, f32[64,16384]{1,0:T(8,128)S(1)} %copy-done.1), kind=kOutput, calls=%fused_computation.1 | convolution fusion | flops 807403520 | bytes 12599296 | tf_op jit(solution)/shard_map/dot_general | solution.py:19
  (64 shorter events, 8.4 us)
Async XLA Ops:
  6.5 150.9 %all-reduce.2.cloned.1.call-start = ((), (), s32[]{:S(2)}) async-start(), calls=%async_computation | async-start | bytes 8388608 | tf_op jit(solution)/shard_map/psum | solution.py:15
  74.5 0.7 copy-start.2
  229.7 7.2 %collective-permute-start = (f32[64,16384]{1,0:T(8,128)S(1)}, f32[64,16384]{1,0:T(8,128)S(1)}, u32[]{:S(2)}, u32[]{:S(2)}) collective-permute-start(f32[64,16384]{1,0:T(8,128)S(1)} %convolution_multiply_fusion), channel_id=1, source_target_pairs={{0,8},{8,0},{16,24},{24,16},{1,9},{9,1},{17,25},{25,17},{2,10},{10... | collective-permute-start | bytes 12582920 | tf_op jit(solution)/shard_map/ppermute | solution.py:53
  237.3 92.7 %collective-permute-start.1 = (f32[64,16384]{1,0:T(8,128)S(1)}, f32[64,16384]{1,0:T(8,128)S(1)}, u32[]{:S(2)}, u32[]{:S(2)}) collective-permute-start(f32[64,16384]{1,0:T(8,128)S(1)} %add.257), channel_id=1, source_target_pairs={{0,16},{8,24},{16,0},{24,8},{1,17},{9,25},{17,1},{25,9},{2,18},{10... | collective-permute-start | bytes 12582920 | tf_op jit(solution)/shard_map/ppermute | solution.py:53
  330.7 2.0 copy-start
  376.3 5.6 %copy-start.1 = (f32[64,16384]{1,0:T(8,128)S(1)}, f32[64,16384]{1,0:T(8,128)}, u32[]{:S(2)}) copy-start(f32[64,16384]{1,0:T(8,128)} %copy-done) | copy-start | bytes 12582916
Sparse Core Ops, SparseCore 0:
  74.7 82.7 all-reduce.1
